TPU v7x, 32 devices: a whole 2x2x4 slice. The times are simulated.
32 devices in a mesh: section: 8 (over z, x), tensor: 2 (over core), dp: 2 (over y).
Axes of the slice: x: 2, y: 2, z: 4, core: 2. Of those that a mesh axis runs over, the one named last changes fastest.
Arguments:
- forward_input: bfloat16 [8, 256, 4096], P('section', 'dp', 'tensor'), may hold values from -6 to 6
- entering_input: bfloat16 [256, 4096], P('dp', 'tensor'), may hold values from -6 to 6
- stored_input: bfloat16 [2, 8, 256, 4096], P(None, 'section', 'dp', 'tensor'), may hold values from -6 to 6
- output_gradient: bfloat16 [8, 256, 4096], P('section', 'dp', 'tensor'), may hold values from -6 to 6
- last_gradient: bfloat16 [256, 4096], P('dp', 'tensor'), may hold values from -6 to 6
- norm_weight: bfloat16 [8, 4096], P('section', 'tensor'), may hold values from 0.25 to 1.75
- frozen_weight: bfloat16 [8, 4096, 4096], P('section', 'dp', 'tensor'), may hold values from -1 to 2
- adapter_down: bfloat16 [8, 4096, 128], P('section', 'tensor'), may hold values from -0.09375 to 0.09375
- adapter_up: bfloat16 [8, 128, 4096], P('section', None, 'tensor'), may hold values from -0.5 to 0.5
- project: bfloat16 [8, 4096, 32], P('section', 'tensor'), may hold values from -0.013671875 to 0.013671875
- example_token_counts: int32 [2, 9, 3], P('dp'), may hold values from 1 to 64, 128 in all within a row
- sketch_owner_rows: int32 [2, 27], P('dp'), may hold values from 0 to 26, each once within a row
Outputs:
- fwd_out: bfloat16 [8, 256, 4096], P('section', 'dp', 'tensor')
- grad_out: bfloat16 [8, 256, 4096], P('section', 'dp', 'tensor')
- sketches: float32 [54, 4096], P('dp', 'section')
Inputs may be any that keep to these rules, and one draw needn't show every extreme that they name: `example_token_counts`: each micro-batch of each replica holds 3 examples whose lengths sum to 128, the longest exactly 64. `sketch_owner_rows`: within each replica every owner row appears exactly once.
All inputs are finite; a program needn't handle non-finite values.
Results may differ from a plain program's by a relative error of at most 0.025.
Values may be sent and summed in bfloat16 or wider, within the bound.
A program may use at most 64 MiB of HBM per device.

v0:
```python
import jax
import jax.numpy as jnp
from jax import lax
from jax.sharding import PartitionSpec as P

MODEL_WIDTH = 4096


ADAPTER_SCALE = 2.0
NORM_EPS = 1e-05


def shifted(value, axis, steps):
    count = lax.axis_size(axis)
    initial, last = (max(0, -steps), min(count, count - steps))
    return lax.ppermute(value, axis, [(source, source + steps) for source in range(initial, last)])


def normalize(hidden, norm_scale):
    wide = hidden.astype(jnp.float32)
    squares = lax.psum(jnp.sum(wide * wide, axis=1), "tensor")
    inv_rms = lax.rsqrt(squares / MODEL_WIDTH + NORM_EPS)[:, None]
    normed = (wide * inv_rms * norm_scale.astype(jnp.float32)[None, :]).astype(jnp.bfloat16)
    return (wide, inv_rms, normed)


def forward_layer(hidden, norm_scale, full_weight, down_factor, up_factor):
    wide, inv_rms, normed = normalize(hidden, norm_scale)
    full_normed = lax.all_gather(normed, "tensor", axis=1, tiled=True)
    adapter_input = lax.psum(
        jnp.dot(normed, down_factor, preferred_element_type=jnp.float32).astype(jnp.bfloat16),
        "tensor",
    )
    frozen_output = jnp.dot(full_normed, full_weight, preferred_element_type=jnp.float32)
    combined_output = frozen_output + ADAPTER_SCALE * jnp.dot(
        adapter_input, up_factor, preferred_element_type=jnp.float32
    )
    return (wide + combined_output).astype(jnp.bfloat16)


def backward_layer(hidden, cotangent, norm_scale, full_weight, down_factor, up_factor, proj):
    wide, inv_rms, normed = normalize(hidden, norm_scale)
    contract_last = (((1,), (1,)), ((), ()))
    adapter_input, adapter_gradient, sketch_cols = (
        lax.psum(
            jnp.dot(normed, down_factor, preferred_element_type=jnp.float32).astype(jnp.bfloat16),
            "tensor",
        ).astype(jnp.float32),
        lax.psum(
            lax.dot_general(
                cotangent, up_factor, contract_last, preferred_element_type=jnp.float32
            ).astype(jnp.bfloat16),
            "tensor",
        ).astype(jnp.float32),
        lax.psum(
            jnp.dot(cotangent, proj, preferred_element_type=jnp.float32).astype(jnp.bfloat16),
            "tensor",
        ).astype(jnp.float32),
    )
    adapter_input = adapter_input.astype(jnp.bfloat16)
    adapter_gradient = adapter_gradient.astype(jnp.bfloat16)
    partials = lax.dot_general(
        cotangent, full_weight, contract_last, preferred_element_type=jnp.float32
    )
    reduced_sum = lax.psum_scatter(
        partials.astype(jnp.bfloat16), "tensor", scatter_dimension=1, tiled=True
    ).astype(jnp.float32)
    normed_gradient = reduced_sum + ADAPTER_SCALE * lax.dot_general(
        adapter_gradient, down_factor, contract_last, preferred_element_type=jnp.float32
    )
    scaled = norm_scale.astype(jnp.float32)[None, :] * normed_gradient
    inner_sum = lax.psum(jnp.sum(wide * scaled, axis=1), "tensor")[:, None] / MODEL_WIDTH
    back = cotangent.astype(jnp.float32) + inv_rms * (scaled - wide * inv_rms * inv_rms * inner_sum)
    return (back.astype(jnp.bfloat16), adapter_input, sketch_cols)


def example_sketch(adapter_input, sketch_cols, example_lengths):
    seg_ends = jnp.cumsum(example_lengths)
    seg_starts = seg_ends - example_lengths
    positions = lax.broadcasted_iota(
        jnp.int32, (adapter_input.shape[0], example_lengths.shape[0]), 0
    )
    member = ((positions >= seg_starts[None, :]) & (positions < seg_ends[None, :])).astype(
        jnp.float32
    )
    masked = (adapter_input.astype(jnp.float32)[:, None, :] * member[:, :, None]).reshape(
        adapter_input.shape[0], -1
    )
    part = lax.dot_general(
        masked,
        sketch_cols,
        (((0,), (0,)), ((), ())),
        precision=lax.Precision.HIGHEST,
        preferred_element_type=jnp.float32,
    )
    return ADAPTER_SCALE * part.reshape(example_lengths.shape[0], -1)


def per_device(
    forward_input,
    entering_input,
    stored_input,
    output_gradient,
    last_gradient,
    norm_weight,
    frozen_weight,
    adapter_down,
    adapter_up,
    project,
    example_token_counts,
    sketch_owner_rows,
):
    sections = lax.axis_size("section")
    section_index = lax.axis_index("section")
    norm_scale = norm_weight[0]
    weight_rows = frozen_weight[0]
    down_factor = adapter_down[0]
    up_factor = adapter_up[0]
    proj = project[0]
    full_weight = lax.all_gather(weight_rows, "dp", axis=0, tiled=True)
    first_out = forward_layer(forward_input[0], norm_scale, full_weight, down_factor, up_factor)
    back_first, adapter_first, cols_first = backward_layer(
        stored_input[0, 0],
        output_gradient[0],
        norm_scale,
        full_weight,
        down_factor,
        up_factor,
        proj,
    )
    arrived = shifted(first_out, "section", 1)
    returned = shifted(back_first, "section", -1)
    entering = jnp.where(section_index == 0, entering_input, arrived)
    upstream = jnp.where(section_index == sections - 1, last_gradient, returned)
    later_output = forward_layer(entering, norm_scale, full_weight, down_factor, up_factor)
    second_backward, adapter_second, cols_second = backward_layer(
        stored_input[1, 0], upstream, norm_scale, full_weight, down_factor, up_factor, proj
    )
    lengths_all = example_token_counts[0]
    batch_count = lengths_all.shape[0]
    seg_count = lengths_all.shape[1]
    lengths_first = lax.dynamic_index_in_dim(lengths_all, section_index, 0, keepdims=False)
    lengths_second = lax.dynamic_index_in_dim(lengths_all, section_index + 1, 0, keepdims=False)
    sketch_first = example_sketch(adapter_first, cols_first, lengths_first)
    sketch_second = example_sketch(adapter_second, cols_second, lengths_second)
    stacked = jnp.concatenate([sketch_first, sketch_second], 0)[None]
    pieces = lax.all_to_all(
        stacked.astype(jnp.bfloat16), "section", split_axis=2, concat_axis=0, tiled=True
    ).astype(stacked.dtype)
    early_part = jnp.pad(pieces[:, :seg_count], ((0, 1), (0, 0), (0, 0)))
    late_part = jnp.pad(pieces[:, seg_count:], ((1, 0), (0, 0), (0, 0)))
    gathered = (early_part + late_part).reshape(batch_count * seg_count, -1)
    row_ids = sketch_owner_rows[0]
    targets = lax.broadcasted_iota(jnp.int32, (row_ids.shape[0], row_ids.shape[0]), 1)
    placement_table = (row_ids[:, None] == targets).astype(jnp.float32)
    sketches = lax.dot_general(
        placement_table,
        gathered,
        (((0,), (0,)), ((), ())),
        precision=lax.Precision.HIGHEST,
        preferred_element_type=jnp.float32,
    )
    return (later_output[None], second_backward[None], sketches)


def solution(mesh):
    placed = (
        P("section", "dp", "tensor"),
        P("dp", "tensor"),
        P(None, "section", "dp", "tensor"),
        P("section", "dp", "tensor"),
        P("dp", "tensor"),
        P("section", "tensor"),
        P("section", "dp", "tensor"),
        P("section", "tensor", None),
        P("section", None, "tensor"),
        P("section", "tensor", None),
        P("dp", None, None),
        P("dp", None),
    )
    return jax.shard_map(
        per_device,
        mesh=mesh,
        in_specs=placed,
        out_specs=(P("section", "dp", "tensor"), P("section", "dp", "tensor"), P("dp", "section")),
        check_vma=False,
    )
```

profile of v0, /device:TPU:8, one launch (start us, length us, event | category | flops | bytes accessed | tf_op | source)
XLA Modules:
  0.0 421.9 jit_solution(1597284383874569747)
XLA Ops:
  7.3 0.7 all-gather.9.cloned.1.call-update
  8.0 201.6 %all-gather.9.cloned.1.call-done = bf16[1,4096,2048]{2,1,0:T(8,128)(2,1)} async-done(((bf16[1,2048,2048]{2,1,0:T(8,128)(2,1)}), bf16[1,4096,2048]{2,1,0:T(8,128)(2,1)}) %all-gather.9.cloned.1.call-update) | async-done | bytes 16777232 | tf_op jit(solution)/shard_map/all_gather | solution.py:120
  209.6 12.6 %fusion.8 = bf16[128,4096]{1,0:T(8,128)(2,1)} fusion(bf16[1,4096,2048]{2,1,0:T(8,128)(2,1)} %all-gather.9.cloned.1.call-done, bf16[1,128,2048]{2,1,0:T(8,128)(2,1)} %param.15), kind=kOutput, calls=%fused_computation.8 | convolution fusion | flops 2148007936 | bytes 18350080 | tf_op jit(solution)/shard_map/dot_general | solution.py:62
  222.2 0.0 all-reduce.11.cloned.1.call-start
  222.3 0.3 convolution_convert_fusion.3
  222.6 3.4 psum.103
  226.1 0.2 fusion.33
  226.3 4.8 %reduce-scatter.3.cloned.1.call-done = bf16[128,2048]{1,0:T(8,128)(2,1)} async-done(((bf16[128,4096]{1,0:T(8,128)(2,1)}), bf16[128,2048]{1,0:T(8,128)(2,1)}) %reduce-scatter.3.cloned.1.call-update) | async-done | bytes 524304 | tf_op jit(solution)/shard_map/reduce_scatter | solution.py:65
  231.1 2.6 fusion.48
  233.7 2.4 all-reduce.3
  236.1 2.4 fusion.44
  238.5 3.3 collective-permute-start.1
  241.9 1.0 convolution_convert_fusion.5
  242.8 11.9 %collective-permute-done.1 = bf16[128,2048]{1,0:T(8,128)(2,1)S(1)} collective-permute-done((bf16[128,2048]{1,0:T(8,128)(2,1)}, bf16[128,2048]{1,0:T(8,128)(2,1)S(1)}, u32[]{:S(2)}, u32[]{:S(2)}) %collective-permute-start.1) | collective-permute-done | bytes 524320 | tf_op jit(solution)/shard_map/ppermute | solution.py:16
  254.7 0.1 broadcast_select_fusion
  254.8 0.9 convolution_convert_fusion.2
  255.7 0.0 reduce-scatter.5.cloned.1.call-start
  255.8 12.4 %fusion.11 = bf16[128,4096]{1,0:T(8,128)(2,1)} fusion(bf16[128,2048]{1,0:T(8,128)(2,1)S(1)} %broadcast_select_fusion, bf16[1,4096,2048]{2,1,0:T(8,128)(2,1)} %all-gather.9.cloned.1.call-done), kind=kOutput, calls=%fused_computation.9 | convolution fusion | flops 2148007936 | bytes 18350080 | tf_op jit(solution)/shard_map/dot_general | solution.py:62
  268.2 0.0 all-gather.5.cloned.1.call-start
  268.2 6.6 %all-reduce.11.cloned.1.call-done = (bf16[128,128]{1,0:T(8,128)(2,1)}, bf16[128,128]{1,0:T(8,128)(2,1)}) async-done(((bf16[128,128]{1,0:T(8,128)(2,1)}, bf16[128,128]{1,0:T(8,128)(2,1)}), (bf16[128,128]{1,0:T(8,128)(2,1)}, bf16[128,128]{1,0:T(8,128)(2,1)})) %all-reduce.11.cloned.1.call-update) | async-done | bytes 65552 | tf_op jit(solution)/shard_map/psum | solution.py:30
  274.8 11.7 %reduce-scatter.5.cloned.1.call-done = bf16[128,2048]{1,0:T(8,128)(2,1)} async-done(((bf16[128,4096]{1,0:T(8,128)(2,1)}), bf16[128,2048]{1,0:T(8,128)(2,1)}) %reduce-scatter.5.cloned.1.call-update) | async-done | bytes 524304 | tf_op jit(solution)/shard_map/reduce_scatter | solution.py:65
  286.5 2.8 fusion.55
  289.3 0.2 all-reduce.9.cloned.1.call-start
  289.6 0.3 dynamic-slice_reduce_fusion.1
  289.8 0.2 reduce-window.15
  290.0 0.2 reduce-window.14
  290.2 0.9 convolution_convert_fusion.7
  291.1 8.6 %all-gather.5.cloned.1.call-done = bf16[128,4096]{1,0:T(8,128)(2,1)} async-done(((bf16[128,2048]{1,0:T(8,128)(2,1)}), bf16[128,4096]{1,0:T(8,128)(2,1)}) %all-gather.5.cloned.1.call-update) | async-done | bytes 1048592 | tf_op jit(solution)/shard_map/all_gather | solution.py:29
  299.7 8.4 %fusion.6 = f32[128,2048]{1,0:T(8,128)S(1)} fusion(bf16[128,4096]{1,0:T(8,128)(2,1)} %all-gather.5.cloned.1.call-done, bf16[1,4096,2048]{2,1,0:T(8,128)(2,1)} %all-gather.9.cloned.1.call-done), kind=kOutput, calls=%fused_computation.6 | convolution fusion | flops 2147483648 | bytes 18874368 | tf_op jit(solution)/shard_map/dot_general | solution.py:34
  308.2 1.1 fusion.20
  309.3 3.4 collective-permute-start
  312.7 0.1 fusion.96
  312.7 2.0 convolution_convert_fusion.1
  314.7 0.9 convolution_convert_fusion.6
  315.6 10.9 %collective-permute-done = bf16[128,2048]{1,0:T(8,128)(2,1)} collective-permute-done((bf16[128,2048]{1,0:T(8,128)(2,1)}, bf16[128,2048]{1,0:T(8,128)(2,1)}, u32[]{:S(2)}, u32[]{:S(2)}) %collective-permute-start) | collective-permute-done | bytes 524320 | tf_op jit(solution)/shard_map/ppermute | solution.py:16
  326.5 1.3 fusion.58
  327.8 2.5 all-reduce.2
  330.3 2.0 convolution_convert_fusion
  332.3 2.6 fusion.63
  334.9 0.9 convolution_convert_fusion.4
  335.9 0.0 all-gather.7.cloned.1.call-start
  335.9 0.1 fusion.94
  336.0 0.6 all-gather.7.cloned.1.call-update
  336.6 18.0 %all-reduce.9.cloned.1.call-done = (bf16[128,128]{1,0:T(8,128)(2,1)}, bf16[128,128]{1,0:T(8,128)(2,1)}, bf16[128,32]{0,1:T(8,128)(2,1)}, bf16[128,128]{1,0:T(8,128)(2,1)}, bf16[128,32]{0,1:T(8,128)(2,1)}) async-done(((bf16[128,128]{1,0:T(8,128)(2,1)}, bf16[128,128]{1,0:T(8,128)(2,1)}, bf16[128,32]{0,1:T(8,128)(2,1)}, bf16[128,128]{1,0:T(8,128)(2,1)}, bf16[128,32]{0,1:T(8,128)(2,1)}), ...) | async-done | bytes 114704 | tf_op jit(solution)/shard_map/psum | solution.py:30
  354.6 0.8 copy.29
  355.5 0.9 fusion.32
  356.5 0.1 copy.30
  356.6 0.1 concatenate.16
  356.7 0.8 copy.27
  357.6 0.9 fusion.31
  358.6 0.1 copy.28
  358.7 0.1 concatenate.15
  358.9 2.9 copy.31
  361.8 0.5 broadcast.126
  362.3 23.5 %reduce.8 = bf16[4096,6]{1,0:T(8,128)(2,1)} reduce(bf16[4096,1,6]{2,1,0:T(2,128)(2,1)S(1)} %bitcast.167, bf16[]{:T(256)} %broadcast.126), dimensions={1}, to_apply=%bitcast.144.reduce_sub_computation | reduce | bytes 98306
  385.8 2.8 reshape.252
  388.5 10.9 %all_to_all.4 = bf16[8,2,1536]{2,1,0:T(2,128)(2,1)S(1)} all-to-all(bf16[8,2,1536]{2,1,0:T(2,128)(2,1)S(1)} %reshape.252), channel_id=1, replica_groups=mesh['section'=8,'tensor'=2,'dp'=2] {'section'}, dimensions={0} | all-to-all | bytes 98304 | tf_op jit(solution)/shard_map/all_to_all | solution.py:147
  399.4 2.3 reshape.253
  401.8 2.3 copy.32
  404.1 0.3 convert_reduce_fusion
  404.4 0.1 copy.36
  404.6 0.9 fusion.91
  405.5 8.4 %fusion.4 = f32[128,2048]{1,0:T(8,128)S(1)} fusion(bf16[128,4096]{1,0:T(8,128)(2,1)} %all-gather.7.cloned.1.call-done, bf16[1,4096,2048]{2,1,0:T(8,128)(2,1)} %all-gather.9.cloned.1.call-done), kind=kOutput, calls=%fused_computation.4 | convolution fusion | flops 2147483648 | bytes 18874368 | tf_op jit(solution)/shard_map/dot_general | solution.py:34
  414.0 1.1 fusion.22
  (54 shorter events, 0.4 us)
Async XLA Ops:
  7.2 223.9 %copy-start = (bf16[1,2048,128]{2,1,0:T(8,128)(2,1)S(1)}, bf16[1,2048,128]{2,1,0:T(8,128)(2,1)}, u32[]{:S(2)}) copy-start(bf16[1,2048,128]{2,1,0:T(8,128)(2,1)} %param.19) | copy-start | bytes 1572868
  7.2 215.1 %copy-start.1 = (bf16[1,128,2048]{2,1,0:T(8,128)(2,1)S(1)}, bf16[1,128,2048]{2,1,0:T(8,128)(2,1)}, u32[]{:S(2)}) copy-start(bf16[1,128,2048]{2,1,0:T(8,128)(2,1)} %param.15) | copy-start | bytes 1572868
  7.2 215.1 %copy-start.13 = (bf16[1,2048]{1,0:T(2,128)(2,1)S(1)}, bf16[1,2048]{1,0:T(2,128)(2,1)}, u32[]{:S(2)}) copy-start(bf16[1,2048]{1,0:T(2,128)(2,1)} %param.17) | copy-start | bytes 12292
  7.2 215.1 %copy-start.2 = (bf16[1,128,2048]{2,1,0:T(8,128)(2,1)S(1)}, bf16[1,128,2048]{2,1,0:T(8,128)(2,1)}, u32[]{:S(2)}) copy-start(bf16[1,128,2048]{2,1,0:T(8,128)(2,1)} %param.20) | copy-start | bytes 1572868
  7.2 218.8 %copy-start.6 = (bf16[1,128,2048]{2,1,0:T(8,128)(2,1)S(1)}, bf16[1,128,2048]{2,1,0:T(8,128)(2,1)}, u32[]{:S(2)}) copy-start(bf16[1,128,2048]{2,1,0:T(8,128)(2,1)} %param.12) | copy-start | bytes 1572868
  7.2 223.8 %copy-start.7 = (bf16[2,1,128,2048]{3,2,1,0:T(8,128)(2,1)S(1)}, bf16[2,1,128,2048]{3,2,1,0:T(8,128)(2,1)}, u32[]{:S(2)}) copy-start(bf16[2,1,128,2048]{3,2,1,0:T(8,128)(2,1)} %param.14) | copy-start | bytes 3145732
  7.2 202.4 %all-gather.9.cloned.1.call-start = ((), (), s32[]{:S(2)}) async-start(), calls=%async_computation.7 | async-start | bytes 25165824 | tf_op jit(solution)/shard_map/all_gather | solution.py:120
  8.0 223.1 %reduce-scatter.3.cloned.1.call-start = ((), (), s32[]{:S(2)}) async-start(), calls=%async_computation.5 | async-start | bytes 1572864 | tf_op jit(solution)/shard_map/reduce_scatter | solution.py:65
  222.2 52.6 %all-reduce.11.cloned.1.call-start = ((), (), s32[]{:S(2)}) async-start(), calls=%async_computation.9 | async-start | bytes 131072 | tf_op jit(solution)/shard_map/psum | solution.py:30
  231.1 58.5 %copy-start.14 = (s32[1,9,3]{1,0,2:T(1,128)S(1)}, s32[1,9,3]{1,0,2:T(1,128)}, u32[]{:S(2)}) copy-start(s32[1,9,3]{1,0,2:T(1,128)} %param.22) | copy-start | bytes 328
  231.1 59.1 %copy-start.10 = (bf16[1,2048,32]{1,2,0:T(8,128)(2,1)S(1)}, bf16[1,2048,32]{1,2,0:T(8,128)(2,1)}, u32[]{:S(2)}) copy-start(bf16[1,2048,32]{1,2,0:T(8,128)(2,1)} %param.21) | copy-start | bytes 393220
  238.5 16.2 %collective-permute-start.1 = (bf16[128,2048]{1,0:T(8,128)(2,1)}, bf16[128,2048]{1,0:T(8,128)(2,1)S(1)}, u32[]{:S(2)}, u32[]{:S(2)}) collective-permute-start(bf16[128,2048]{1,0:T(8,128)(2,1)} %fusion.44), channel_id=1, source_target_pairs={{4,0},{8,4},{12,8},{16,12},{20,16},{24,20},{28,24},{5,1},{9,5},{13... | collective-permute-start | bytes 1572872 | tf_op jit(solution)/shard_map/ppermute | solution.py:16
  255.7 30.8 %reduce-scatter.5.cloned.1.call-start = ((), (), s32[]{:S(2)}) async-start(), calls=%async_computation.6 | async-start | bytes 1572864 | tf_op jit(solution)/shard_map/reduce_scatter | solution.py:65
  268.2 31.5 %all-gather.5.cloned.1.call-start = ((), (), s32[]{:S(2)}) async-start(), calls=%async_computation.3 | async-start | bytes 1572864 | tf_op jit(solution)/shard_map/all_gather | solution.py:29
  274.8 33.3 %copy-start.12 = (bf16[128,128]{1,0:T(8,128)(2,1)S(1)}, bf16[128,128]{1,0:T(8,128)(2,1)}, u32[]{:S(2)}) copy-start(bf16[128,128]{1,0:T(8,128)(2,1)} %get-tuple-element.19) | copy-start | bytes 98308
  289.3 43.0 %copy-start.8 = (bf16[128,2048]{1,0:T(8,128)(2,1)S(1)}, bf16[128,2048]{1,0:T(8,128)(2,1)}, u32[]{:S(2)}) copy-start(bf16[128,2048]{1,0:T(8,128)(2,1)} %reduce-scatter.5.cloned.1.call-done) | copy-start | bytes 1572868
  289.3 65.3 %all-reduce.9.cloned.1.call-start = ((), (), s32[]{:S(2)}) async-start(), calls=%async_computation.8 | async-start | bytes 229376 | tf_op jit(solution)/shard_map/psum | solution.py:30
  291.1 35.4 %copy-start.9 = (bf16[128,2048]{1,0:T(8,128)(2,1)S(1)}, bf16[128,2048]{1,0:T(8,128)(2,1)}, u32[]{:S(2)}) copy-start(bf16[128,2048]{1,0:T(8,128)(2,1)} %param.13) | copy-start | bytes 1572868
  308.1 96.4 %copy-start.15 = (s32[1,27]{1,0:T(1,128)S(1)}, s32[1,27]{1,0:T(1,128)}, u32[]{:S(2)}) copy-start(s32[1,27]{1,0:T(1,128)} %param.23) | copy-start | bytes 328
  309.3 17.2 %collective-permute-start = (bf16[128,2048]{1,0:T(8,128)(2,1)}, bf16[128,2048]{1,0:T(8,128)(2,1)}, u32[]{:S(2)}, u32[]{:S(2)}) collective-permute-start(bf16[128,2048]{1,0:T(8,128)(2,1)} %fusion.20), channel_id=1, source_target_pairs={{0,4},{4,8},{8,12},{12,16},{16,20},{20,24},{24,28},{1,5},{5,9},{9,... | collective-permute-start | bytes 1572872 | tf_op jit(solution)/shard_map/ppermute | solution.py:16
  327.8 31.0 %copy-start.4 = (bf16[128,2048]{1,0:T(8,128)(2,1)}, bf16[128,2048]{1,0:T(8,128)(2,1)S(1)}, u32[]{:S(2)}) copy-start(bf16[128,2048]{1,0:T(8,128)(2,1)S(1)} %get-tuple-element.22) | copy-start | bytes 1572868
  334.9 1.1 copy-start.3
  335.9 69.7 %all-gather.7.cloned.1.call-start = ((), (), s32[]{:S(2)}) async-start(), calls=%async_computation.4 | async-start | bytes 1572864 | tf_op jit(solution)/shard_map/all_gather | solution.py:29
  362.3 51.7 %copy-start.11 = (bf16[128,128]{1,0:T(8,128)(2,1)S(1)}, bf16[128,128]{1,0:T(8,128)(2,1)}, u32[]{:S(2)}) copy-start(bf16[128,128]{1,0:T(8,128)(2,1)} %get-tuple-element.14) | copy-start | bytes 98308
  404.1 9.9 %copy-start.5 = (bf16[128,2048]{1,0:T(8,128)(2,1)S(1)}, bf16[128,2048]{1,0:T(8,128)(2,1)}, u32[]{:S(2)}) copy-start(bf16[128,2048]{1,0:T(8,128)(2,1)} %copy-done.4) | copy-start | bytes 1572868
Sparse Core Ops, SparseCore 0:
  9.6 199.9 all-gather.8
  222.4 8.6 reduce-scatter.2
  255.8 18.9 all-reduce.10
  276.9 9.5 reduce-scatter.4
  289.4 10.2 all-gather.4
  336.0 18.6 all-reduce.8
  356.8 10.1 all-gather.6
where the time goes:
time: 426 us; the launch traced here: 422 us
  waiting for transfers between devices  275 us (65%)
  matrix products  61.1 us (14%)
  other arithmetic  30.9 us (7%)
  blocking collectives  19.2 us (5%)
  between operations  14.5 us (3%)
  local copies, waits for them, and re-layouts  13.5 us (3%)
  starting transfers between devices  7.14 us (2%)
    all_gather x1, waiting for transfers between devices, per_device(): full_weight = lax.all_gather(weight_rows, 'dp', axis=0, tiled=True)  202 us
    dot_general x2, matrix products, backward_layer(): lax.dot_general(cotangent, full_weight, contract_last, preferred_element_...  25 us
    psum x2, waiting for transfers between devices, forward_layer(): lax.psum(jnp.dot(normed, down_factor, preferred_element_type=jnp.float32)...  24.6 us
    unnamed x1, other arithmetic  23.5 us
    ppermute x2, waiting for transfers between devices, shifted(): lax.ppermute(value, axis, [(source, source + steps) for source in range(i...  22.7 us
    dot_general x2, matrix products, forward_layer(): jnp.dot(full_normed, full_weight, preferred_element_type=jnp.float32)  16.9 us
    reduce_scatter x2, waiting for transfers between devices, backward_layer(): lax.psum_scatter(partials.astype(jnp.bfloat16), 'tensor', scatter_dimensi...  16.5 us
    all_to_all x1, blocking collectives, per_device(): lax.all_to_all(stacked.astype(jnp.bfloat16), 'section', split_axis=2, con...  10.9 us
  transfers between devices with their start and end apart: 9, of which 8 were waited for; matrix products, arithmetic and copies ran while one was open for 14% of the time, Pallas kernels for 0%

commit v1 on v0

--- a/solution.py
+++ b/solution.py
@@ -1,6 +1,10 @@
+import functools
+
 import jax
 import jax.numpy as jnp
 from jax import lax
+from jax.experimental import pallas as pl
+from jax.experimental.pallas import tpu as pltpu
 from jax.sharding import PartitionSpec as P
 
 MODEL_WIDTH = 4096
@@ -163,6 +167,684 @@
     return (later_output[None], second_backward[None], sketches)
 
 
+MESH = pl.DeviceIdType.MESH
+CONTRACT_LAST = (((1,), (1,)), ((), ()))
+ROWS = 16
+TILE = 256
+
+COPIES = (
+    "norm",
+    "down",
+    "up",
+    "proj",
+    "h1",
+    "g1",
+    "s1",
+    "s2",
+    "last",
+    "g1y",
+    "shift_f",
+    "shift_b0",
+    "shift_b1",
+    "h2",
+    "g20",
+    "g21",
+    "g2y0",
+    "g2y1",
+    "nin1",
+    "nfw1",
+    "nin2",
+    "nfw2",
+    "fa1",
+    "fb1",
+    "fa2",
+    "fb2",
+    "pb1",
+    "pb2",
+    "po1",
+    "po2",
+    "dn1",
+    "dn2",
+    "back",
+)
+
+
+def window_kernel(
+    sections,
+    h_in,
+    enter_in,
+    stored_in,
+    g_in,
+    last_in,
+    norm_in,
+    w_in,
+    down_in,
+    up_in,
+    proj_in,
+    counts,
+    owners,
+    out_f,
+    out_b,
+    out_s,
+    w,
+    nwf,
+    downf,
+    upf,
+    projf,
+    h1f,
+    h2f,
+    s1f,
+    s2f,
+    g1f,
+    g2f,
+    g1o,
+    g2o,
+    normed,
+    scratch_n,
+    other_in,
+    f_send,
+    f_recv,
+    f_own,
+    o1,
+    pb,
+    pbr,
+    po,
+    por,
+    sb,
+    dn,
+    lora,
+    bk,
+    bkr,
+    inv_f,
+    inv_1,
+    inv_2,
+    sk,
+    skr,
+    send_sem,
+    recv_sem,
+    sk_send,
+    sk_recv,
+    local_sem,
+):
+    s, t, d = lax.axis_index("section"), lax.axis_index("tensor"), lax.axis_index("dp")
+    tokens, width = h_in.shape
+    half = tokens // 2
+    features = 2 * width
+    segs = counts.shape[1]
+    final = sections - 1
+    other_t, other_d = 1 - t, 1 - d
+    partner = {"tensor": other_t}
+    peer = {"dp": other_d}
+    cross = {"tensor": other_t, "dp": other_d}
+    mine = pl.ds(pl.multiple_of(t * half, half), half)
+    theirs = pl.ds(pl.multiple_of(other_t * half, half), half)
+
+    def remote(name, src, dst, device, tick=None):
+        index = COPIES.index(name if tick is None else name + str(tick))
+        return pltpu.make_async_remote_copy(
+            src_ref=src,
+            dst_ref=dst,
+            send_sem=send_sem.at[index],
+            recv_sem=recv_sem.at[index],
+            device_id=device,
+            device_id_type=MESH,
+        )
+
+    def f32(value):
+        return value.astype(jnp.float32)
+
+    local = [
+        pltpu.make_async_copy(src, dst, local_sem.at[i])
+        for i, (src, dst) in enumerate(
+            [
+                (h_in, h1f.at[t]),
+                (norm_in, nwf.at[t]),
+                (stored_in.at[0], s1f.at[t]),
+                (g_in, g1f.at[t]),
+                (down_in, downf.at[t]),
+                (up_in, upf.at[t]),
+                (proj_in, projf.at[t]),
+                (stored_in.at[1], s2f.at[t]),
+                (w_in, w),
+            ]
+        )
+    ]
+    for copy in local:
+        copy.start()
+    enter_copy = pltpu.make_async_copy(enter_in, h2f.at[t], local_sem.at[9])
+    last_copy = pltpu.make_async_copy(last_in, g2f.at[t], local_sem.at[10])
+
+    @pl.when(s == 0)
+    def _():
+        enter_copy.start()
+
+    @pl.when(s == final)
+    def _():
+        last_copy.start()
+
+    barrier = pltpu.get_barrier_semaphore()
+    for device in (partner, peer, cross):
+        pl.semaphore_signal(barrier, inc=1, device_id=device, device_id_type=MESH)
+    for step in range(1, sections):
+        pl.semaphore_signal(
+            barrier,
+            inc=1,
+            device_id={"section": lax.rem(s + step, sections)},
+            device_id_type=MESH,
+        )
+    pl.semaphore_wait(barrier, 3 + sections - 1)
+
+    g1y = remote("g1y", g_in, g1o, peer)
+    h1c = remote("h1", h_in, h1f.at[t], partner)
+    normc = remote("norm", norm_in, nwf.at[t], partner)
+    s1c = remote("s1", stored_in.at[0], s1f.at[t], partner)
+    downc = remote("down", down_in, downf.at[t], partner)
+    g1c = remote("g1", g_in, g1f.at[t], partner)
+    upc = remote("up", up_in, upf.at[t], partner)
+    projc = remote("proj", proj_in, projf.at[t], partner)
+    s2c = remote("s2", stored_in.at[1], s2f.at[t], partner)
+    early = [h1c, normc, g1y, s1c, downc, g1c, upc, projc, s2c]
+    for copy in early:
+        copy.start()
+    lastc = remote("last", last_in, g2f.at[t], partner)
+
+    @pl.when(s == final)
+    def _():
+        lastc.start()
+
+    def normalize_into(hidden, inv, dst):
+        def body(i, carry):
+            rows = pl.ds(pl.multiple_of(i * ROWS, ROWS), ROWS)
+            total = jnp.zeros((ROWS, 1), jnp.float32)
+            for b in range(2):
+                wide = f32(hidden[b, rows, :])
+                total = total + jnp.sum(wide * wide, axis=1, keepdims=True)
+            scale = lax.rsqrt(total / features + NORM_EPS)
+            inv[rows, :] = jnp.broadcast_to(scale, (ROWS, inv.shape[1]))
+            for b in range(2):
+                dst[b, rows, :] = (f32(hidden[b, rows, :]) * scale * f32(nwf[b])).astype(
+                    jnp.bfloat16
+                )
+            return carry
+
+        lax.fori_loop(0, tokens // ROWS, body, 0)
+
+    def both(lhs, rhs):
+        return (
+            jnp.dot(lhs[0], rhs[0], preferred_element_type=jnp.float32)
+            + jnp.dot(lhs[1], rhs[1], preferred_element_type=jnp.float32)
+        )
+
+    def forward_send(hidden, inv, tick):
+        normalize_into(hidden, inv, normed)
+        copy = remote("nin", normed.at[other_d, mine], other_in.at[tick - 1, mine], peer, tick)
+        copy.start()
+        return copy
+
+    def forward_relay(copy, tick):
+        copy.wait_recv()
+        part = other_in.at[tick - 1, mine]
+        relay = remote("nfw", part, part, partner, tick)
+        relay.start()
+        return relay
+
+    def forward_other(relay, tick):
+        relay.wait_recv()
+        copies = []
+        for name, first in (("fa", 0), ("fb", width // 2)):
+
+            def body(n, carry, first=first):
+                cols = pl.ds(pl.multiple_of(first + n * TILE, TILE), TILE)
+                f_send[tick - 1, :, cols] = jnp.dot(
+                    other_in[tick - 1], w[:, cols], preferred_element_type=jnp.float32
+                ).astype(jnp.bfloat16)
+                return carry
+
+            lax.fori_loop(0, width // 2 // TILE, body, 0)
+            cols = pl.ds(first, width // 2)
+            copy = remote(
+                name, f_send.at[tick - 1, :, cols], f_recv.at[tick - 1, :, cols], peer, tick
+            )
+            copy.start()
+            copies.append(copy)
+        return copies
+
+    def forward_own(hidden, adapter):
+        def body(n, carry):
+            cols = pl.ds(pl.multiple_of(n * TILE, TILE), TILE)
+            f_own[:, cols] = (
+                f32(hidden[t, :, cols])
+                + jnp.dot(normed[d], w[:, cols], preferred_element_type=jnp.float32)
+                + ADAPTER_SCALE
+                * jnp.dot(adapter, upf[t, :, cols], preferred_element_type=jnp.float32)
+            )
+            return carry
+
+        lax.fori_loop(0, width // TILE, body, 0)
+
+    def forward_finish(copies, dst, tick):
+        for part, copy in enumerate(copies):
+            copy.wait_recv()
+            cols = pl.ds(part * (width // 2), width // 2)
+
+            def body(i, carry, cols=cols):
+                rows = pl.ds(pl.multiple_of(i * ROWS, ROWS), ROWS)
+                dst[rows, cols] = (
+                    f_own[rows, cols] + f32(f_recv[tick - 1, rows, cols])
+                ).astype(jnp.bfloat16)
+                return carry
+
+            lax.fori_loop(0, tokens // ROWS, body, 0)
+
+    def backward_product(load, dst):
+        def body(n, carry):
+            rows = pl.ds(pl.multiple_of(n * TILE, TILE), TILE)
+            dst[:, rows] = lax.dot_general(
+                load(), w[rows, :], CONTRACT_LAST, preferred_element_type=jnp.float32
+            ).astype(jnp.bfloat16)
+            return carry
+
+        lax.fori_loop(0, w.shape[0] // TILE, body, 0)
+
+    def add_halves(whole, received, store):
+        def body(i, carry):
+            rows = pl.ds(pl.multiple_of(i * ROWS, ROWS), ROWS)
+            full = pl.ds(pl.multiple_of(t * half + i * ROWS, ROWS), ROWS)
+            store(rows, (f32(whole[full, :]) + f32(received[rows, :])).astype(jnp.bfloat16))
+            return carry
+
+        lax.fori_loop(0, half // ROWS, body, 0)
+
+    def backward_other(cotangent, tick):
+        k = tick - 1
+        backward_product(lambda: cotangent[...], pb.at[k])
+        copy = remote("pb", pb.at[k, theirs], pbr.at[k], partner, tick)
+        copy.start()
+        return copy
+
+    def backward_send(copy, tick):
+        k = tick - 1
+        copy.wait_recv()
+
+        def store(rows, value):
+            sb[k, rows, :] = value
+
+        add_halves(pb.at[k], pbr.at[k], store)
+        out = remote("dn", sb.at[k], dn.at[k, d], peer, tick)
+        out.start()
+        return out
+
+    def backward_own(cotangent, tick):
+        k = tick - 1
+        backward_product(lambda: cotangent[t], po.at[k])
+        copy = remote("po", po.at[k, theirs], por.at[k], partner, tick)
+        copy.start()
+        return copy
+
+    def low_rank(cotangent, tick):
+        gradient = (
+            lax.dot_general(
+                cotangent[0], upf[0], CONTRACT_LAST, preferred_element_type=jnp.float32
+            )
+            + lax.dot_general(
+                cotangent[1], upf[1], CONTRACT_LAST, preferred_element_type=jnp.float32
+            )
+        ).astype(jnp.bfloat16)
+        part = jnp.where(t == 0, gradient[:half], gradient[half:])
+        for b in range(2):
+
+            def body(n, carry, b=b):
+                cols = pl.ds(pl.multiple_of(n * TILE, TILE), TILE)
+                lora[b, :, cols] = ADAPTER_SCALE * lax.dot_general(
+                    part, downf[b, cols, :], CONTRACT_LAST, preferred_element_type=jnp.float32
+                )
+                return carry
+
+            lax.fori_loop(0, width // TILE, body, 0)
+        return lax.dot_general(
+            cotangent[0], projf[0], CONTRACT_LAST, preferred_element_type=jnp.float32
+        ) + lax.dot_general(
+            cotangent[1], projf[1], CONTRACT_LAST, preferred_element_type=jnp.float32
+        )
+
+    def backward_finish(copy_own, copy_dn, hidden, inv, cotangent, dst, tick):
+        k = tick - 1
+        copy_own.wait_recv()
+
+        def store(rows, value):
+            dn[k, d, rows, :] = value
+
+        add_halves(po.at[k], por.at[k], store)
+        copy_dn.wait_recv()
+
+        def body(i, carry):
+            rows = pl.ds(pl.multiple_of(i * ROWS, ROWS), ROWS)
+            full = pl.ds(pl.multiple_of(t * half + i * ROWS, ROWS), ROWS)
+            scale = inv[full, :][:, :1]
+            total = jnp.zeros((ROWS, 1), jnp.float32)
+            for b in range(2):
+                scaled = f32(nwf[b]) * (f32(dn[k, b, rows, :]) + lora[b, rows, :])
+                lora[b, rows, :] = scaled
+                total = total + jnp.sum(f32(hidden[b, full, :]) * scaled, axis=1, keepdims=True)
+            factor = scale * scale * (total / features)
+            for b in range(2):
+                dst[b, rows, :] = (
+                    f32(cotangent[b, full, :])
+                    + scale * (lora[b, rows, :] - f32(hidden[b, full, :]) * factor)
+                ).astype(jnp.bfloat16)
+            return carry
+
+        lax.fori_loop(0, half // ROWS, body, 0)
+
+    def sketch(adapter, cols, tick):
+        ranks, width_k = adapter.shape[1], cols.shape[1]
+        piece = sk.shape[2]
+        row = lax.broadcasted_iota(jnp.int32, (8, tokens), 0)
+        place = lax.broadcasted_iota(jnp.int32, (8, tokens), 1)
+        member = jnp.zeros((8, tokens), jnp.float32)
+        start = jnp.int32(0)
+        for j in range(segs):
+            stop = start + counts[0, j, s + tick - 1]
+            inside = (row == (tick - 1) * segs + j) & (place >= start) & (place < stop)
+            member = member + jnp.where(inside, ADAPTER_SCALE, 0.0)
+            start = stop
+        member = member.astype(jnp.bfloat16)
+        col_k = lax.broadcasted_iota(jnp.int32, (width_k, piece), 1)
+        row_k = lax.broadcasted_iota(jnp.int32, (width_k, piece), 0)
+        spread = (lax.rem(col_k, width_k) == row_k).astype(jnp.float32).astype(jnp.bfloat16)
+        wide_cols = jnp.dot(
+            cols.astype(jnp.bfloat16), spread, preferred_element_type=jnp.float32
+        )
+        row_r = lax.broadcasted_iota(jnp.int32, (ranks, piece), 0)
+        col_r = lax.broadcasted_iota(jnp.int32, (ranks, piece), 1)
+
+        for o in range(sections):
+            first = o * (piece // width_k)
+            pick = (row_r == first + lax.div(col_r, width_k)).astype(jnp.float32)
+            wide = jnp.dot(adapter, pick.astype(jnp.bfloat16), preferred_element_type=jnp.float32)
+            value = jnp.dot(
+                member, (wide * wide_cols).astype(jnp.bfloat16), preferred_element_type=jnp.float32
+            )
+            sk[o] = value if tick == 1 else sk[o] + value
+
+    local[0].wait()
+    local[1].wait()
+    normc.wait_recv()
+    h1c.wait_recv()
+    nin1 = forward_send(h1f, inv_f, 1)
+    local[2].wait()
+    s1c.wait_recv()
+    normalize_into(s1f, inv_1, scratch_n)
+    local[4].wait()
+    downc.wait_recv()
+    adapter_f1 = both(normed, downf).astype(jnp.bfloat16)
+    adapter_s1 = both(scratch_n, downf).astype(jnp.bfloat16)
+    for i in (3, 5, 6):
+        local[i].wait()
+    g1c.wait_recv()
+    upc.wait_recv()
+    projc.wait_recv()
+    cols1 = low_rank(g1f, 1)
+    local[8].wait()
+    g1y.wait_recv()
+    pb1 = backward_other(g1o, 1)
+    nfw1 = forward_relay(nin1, 1)
+    dn1 = backward_send(pb1, 1)
+    fout1 = forward_other(nfw1, 1)
+    po1 = backward_own(g1f, 1)
+    backward_finish(po1, dn1, s1f, inv_1, g1f, bk, 1)
+    down_stream = {"section": lax.rem(s + final, sections)}
+    shift_b = [
+        remote("shift_b", bk.at[b], g2f.at[b, mine], down_stream, b) for b in range(2)
+    ]
+
+    @pl.when(s > 0)
+    def _():
+        for copy in shift_b:
+            copy.start()
+
+    forward_own(h1f, adapter_f1)
+    sketch(adapter_s1, cols1, 1)
+    forward_finish(fout1, o1, 1)
+    shift_f = remote("shift_f", o1, h2f.at[t], {"section": lax.rem(s + 1, sections)})
+
+    @pl.when(s < final)
+    def _():
+        shift_f.start()
+
+    @pl.when(s == final)
+    def _():
+        last_copy.wait()
+        lastc.wait_recv()
+
+    g2c = [
+        remote("g2", g2f.at[b, mine], g2f.at[b, mine], partner, b) for b in range(2)
+    ]
+    first_y = COPIES.index("g2y0")
+    g2y = [
+        pltpu.make_async_remote_copy(
+            src_ref=g2f.at[b, mine],
+            dst_ref=g2o.at[mine],
+            send_sem=send_sem.at[first_y + b],
+            recv_sem=recv_sem.at[first_y + t],
+            device_id={"dp": other_d, "tensor": b},
+            device_id_type=MESH,
+        )
+        for b in range(2)
+    ]
+    for b in range(2):
+
+        @pl.when(s < final)
+        def _(b=b):
+            shift_b[b].wait_recv()
+
+        g2y[b].start()
+
+        @pl.when(s < final)
+        def _(b=b):
+            g2c[b].start()
+
+    local[7].wait()
+    s2c.wait_recv()
+    normalize_into(s2f, inv_2, scratch_n)
+    adapter_s2 = both(scratch_n, downf).astype(jnp.bfloat16)
+
+    @pl.when(s < final)
+    def _():
+        for copy in g2c:
+            copy.wait_recv()
+
+    @pl.when(s > 0)
+    def _():
+        for copy in shift_b:
+            copy.wait_send()
+
+    cols2 = low_rank(g2f, 2)
+    nin1.wait_send()
+
+    @pl.when(s > 0)
+    def _():
+        shift_f.wait_recv()
+
+    @pl.when(s == 0)
+    def _():
+        enter_copy.wait()
+
+    h2c = remote("h2", h2f.at[t], h2f.at[t], partner)
+    h2c.start()
+    h2c.wait_recv()
+    nin2 = forward_send(h2f, inv_f, 2)
+    adapter_f2 = both(normed, downf).astype(jnp.bfloat16)
+    for b in range(2):
+        pltpu.make_async_remote_copy(
+            src_ref=g2f.at[b, mine],
+            dst_ref=g2o.at[pl.ds(b * half, half)],
+            send_sem=send_sem.at[first_y + b],
+            recv_sem=recv_sem.at[first_y + b],
+            device_id=peer,
+            device_id_type=MESH,
+        ).wait_recv()
+    pb2 = backward_other(g2o, 2)
+    nfw2 = forward_relay(nin2, 2)
+    dn2 = backward_send(pb2, 2)
+    fout2 = forward_other(nfw2, 2)
+    po2 = backward_own(g2f, 2)
+    sketch(adapter_s2, cols2, 2)
+    sk_copies = []
+    for step in range(1, sections):
+        owner = lax.rem(s + step, sections)
+        copy = pltpu.make_async_remote_copy(
+            src_ref=sk.at[owner],
+            dst_ref=skr.at[s],
+            send_sem=sk_send.at[step],
+            recv_sem=sk_recv.at[step],
+            device_id={"section": owner},
+            device_id_type=MESH,
+        )
+        copy.start()
+        sk_copies.append(copy)
+    skr[s] = sk[s]
+
+    backward_finish(po2, dn2, s2f, inv_2, g2f, bk, 2)
+    back = remote("back", bk.at[other_t], bkr, partner)
+    back.start()
+    forward_own(h2f, adapter_f2)
+    out_b[mine, :] = bk[t]
+
+    for copy in sk_copies:
+        copy.wait_recv()
+    batches = owners.shape[1]
+    own_row = lax.broadcasted_iota(jnp.int32, (batches, batches), 0)
+    onehot = (own_row == owners[...]).astype(jnp.float32)
+    from_row = lax.broadcasted_iota(jnp.int32, (batches, 8 * sections), 0)
+    from_col = lax.broadcasted_iota(jnp.int32, (batches, 8 * sections), 1)
+    entry = lax.rem(from_col, 8)
+    source = (
+        (from_row == segs * lax.div(from_col, 8) + entry) & (entry < 2 * segs)
+    ).astype(jnp.float32)
+    table = jnp.dot(onehot, source, preferred_element_type=jnp.float32)
+    out_s[...] = jnp.dot(
+        table,
+        skr[...].reshape(8 * sections, -1),
+        precision=lax.Precision.HIGHEST,
+        preferred_element_type=jnp.float32,
+    )
+    back.wait_recv()
+    out_b[theirs, :] = bkr[...]
+    forward_finish(fout2, out_f, 2)
+
+    for copy in early + sk_copies + [
+        h2c, nfw1, nin2, nfw2, pb1, pb2, dn1, dn2, po1, po2, back
+    ] + fout1 + fout2 + g2y:
+        copy.wait_send()
+
+    @pl.when(s < final)
+    def _():
+        shift_f.wait_send()
+        for copy in g2c:
+            copy.wait_send()
+
+    @pl.when(s == final)
+    def _():
+        lastc.wait_send()
+
+
+def stationary(
+    forward_input,
+    entering_input,
+    stored_input,
+    output_gradient,
+    last_gradient,
+    norm_weight,
+    frozen_weight,
+    adapter_down,
+    adapter_up,
+    project,
+    example_token_counts,
+    sketch_owner_rows,
+):
+    sections = lax.axis_size("section")
+    _, tokens, width = forward_input.shape
+    rows = frozen_weight.shape[1]
+    ranks, sketch_k = adapter_down.shape[2], project.shape[2]
+    piece = ranks * sketch_k // sections
+    half = tokens // 2
+    bf, f = jnp.bfloat16, jnp.float32
+    anywhere = pl.BlockSpec(memory_space=pl.ANY)
+    vmem = pl.BlockSpec(memory_space=pltpu.VMEM)
+    smem = pl.BlockSpec(memory_space=pltpu.SMEM)
+    full = pltpu.VMEM((2, tokens, width), bf)
+    outs = pl.pallas_call(
+        functools.partial(window_kernel, sections),
+        out_shape=(
+            jax.ShapeDtypeStruct((tokens, width), bf),
+            jax.ShapeDtypeStruct((tokens, width), bf),
+            jax.ShapeDtypeStruct((sketch_owner_rows.shape[1], piece), f),
+        ),
+        in_specs=[anywhere] * 10 + [smem, vmem],
+        out_specs=(vmem, vmem, vmem),
+        scratch_shapes=[
+            pltpu.VMEM((rows, width), bf),
+            pltpu.VMEM((2, 1, width), bf),
+            pltpu.VMEM((2, width, ranks), bf),
+            pltpu.VMEM((2, ranks, width), bf),
+            pltpu.VMEM((2, sketch_k, width), bf),
+            full,
+            full,
+            full,
+            full,
+            full,
+            full,
+            pltpu.VMEM((tokens, width), bf),
+            pltpu.VMEM((tokens, width), bf),
+            full,
+            full,
+            full,
+            full,
+            full,
+            pltpu.VMEM((tokens, width), f),
+            pltpu.VMEM((tokens, width), bf),
+            full,
+            pltpu.VMEM((2, half, width), bf),
+            full,
+            pltpu.VMEM((2, half, width), bf),
+            pltpu.VMEM((2, half, width), bf),
+            pltpu.VMEM((2, 2, half, width), bf),
+            pltpu.VMEM((2, half, width), f),
+            pltpu.VMEM((2, half, width), bf),
+            pltpu.VMEM((half, width), bf),
+            pltpu.VMEM((tokens, 128), f),
+            pltpu.VMEM((tokens, 128), f),
+            pltpu.VMEM((tokens, 128), f),
+            pltpu.VMEM((sections, 8, piece), f),
+            pltpu.VMEM((sections, 8, piece), f),
+            pltpu.SemaphoreType.DMA((len(COPIES),)),
+            pltpu.SemaphoreType.DMA((len(COPIES),)),
+            pltpu.SemaphoreType.DMA((sections,)),
+            pltpu.SemaphoreType.DMA((sections,)),
+            pltpu.SemaphoreType.DMA((11,)),
+        ],
+        compiler_params=pltpu.CompilerParams(
+            collective_id=0, has_side_effects=True, vmem_limit_bytes=60 * 1024 * 1024
+        ),
+        name="window",
+    )(
+        forward_input[0],
+        entering_input,
+        stored_input[:, 0],
+        output_gradient[0],
+        last_gradient,
+        norm_weight,
+        frozen_weight[0],
+        adapter_down[0],
+        adapter_up[0],
+        project[0].T,
+        jnp.swapaxes(example_token_counts, 1, 2),
+        sketch_owner_rows,
+    )
+    return outs[0][None], outs[1][None], outs[2]
+
+
 def solution(mesh):
     placed = (
         P("section", "dp", "tensor"),
@@ -178,8 +860,10 @@
         P("dp", None, None),
         P("dp", None),
     )
+    shape = mesh.shape
+    fits = shape['tensor'] == 2 and shape['dp'] == 2 and shape['section'] > 1
     return jax.shard_map(
-        per_device,
+        stationary if fits else per_device,
         mesh=mesh,
         in_specs=placed,
         out_specs=(P("section", "dp", "tensor"), P("section", "dp", "tensor"), P("dp", "section")),

time: 426 us -> 101 us (0.24)
  waiting for transfers between devices: 275 us -> 0 us
  Pallas kernels: 0 us -> 93.1 us
  matrix products: 61.1 us -> 0 us
  other arithmetic: 30.9 us -> 0 us
  blocking collectives: 19.2 us -> 0 us
  between operations: 14.5 us -> 0.64 us
  starting transfers between devices: 7.14 us -> 0 us
  local copies, waits for them, and re-layouts: 13.5 us -> 6.49 us
    all_gather x3 -> x0, waiting for transfers between devices: 210 us -> none  [the longest x1 202 us: per_device(): full_weight = lax.all_gather(weight_rows, 'dp', axis=0, tiled=True)]
    pallas_call x0 -> x1, Pallas kernels: none -> 93.1 us  [stationary(): pl.pallas_call(functools.partial(window_kernel, sections), out_shape=(jax...]
    dot_general x19 -> x0, matrix products: 61.1 us -> none  [the longest x2 25 us: backward_layer(): lax.dot_general(cotangent, full_weight, contract_last, preferred_element_...]
    psum x2 -> x0, waiting for transfers between devices: 24.6 us -> none  [forward_layer(): lax.psum(jnp.dot(normed, down_factor, preferred_element_type=jnp.float32)...]
    unnamed x1 -> x0, other arithmetic: 23.5 us -> none
    ppermute x2 -> x0, waiting for transfers between devices: 22.7 us -> none  [shifted(): lax.ppermute(value, axis, [(source, source + steps) for source in range(i...]
    reduce_scatter x2 -> x0, waiting for transfers between devices: 16.5 us -> none  [backward_layer(): lax.psum_scatter(partials.astype(jnp.bfloat16), 'tensor', scatter_dimensi...]
    all_to_all x1 -> x0, blocking collectives: 10.9 us -> none  [per_device(): lax.all_to_all(stacked.astype(jnp.bfloat16), 'section', split_axis=2, con...]
  transfers between devices with their start and end apart: 9 -> 0, of which waited for: 8 -> 0; matrix products, arithmetic and copies ran while one was open for 14% -> 0% of each run, Pallas kernels for 0% -> 0%
where the time goes in v1:
time: 101 us; the launch traced here: 100 us
  Pallas kernels  93.1 us (92%)
  local copies, waits for them, and re-layouts  6.49 us (6%)
    pallas_call x1, Pallas kernels, stationary(): pl.pallas_call(functools.partial(window_kernel, sections), out_shape=(jax...  93.1 us
    unnamed x4, local copies, waits for them, and re-layouts  6.49 us

profile of v1, /device:TPU:8, one launch (start us, length us, event | category | flops | bytes accessed | tf_op | source)
XLA Modules:
  0.0 100.3 jit_solution(6114961971577207878)
XLA Ops:
  0.6 1.3 %copy.17 = s32[1,9,3]{1,2,0:T(4,128)} copy(s32[1,9,3]{1,0,2:T(1,128)} %param.22) | data formatting | bytes 216 | tf_op args[10]
  1.9 93.1 %window.1 = (bf16[128,2048]{1,0:T(8,128)(2,1)}, bf16[128,2048]{1,0:T(8,128)(2,1)}, f32[27,512]{1,0:T(8,128)}) custom-call(bf16[128,2048]{1,0:T(8,128)(2,1)} %bitcast.16, bf16[128,2048]{1,0:T(8,128)(2,1)} %enter_in.1, bf16[2,128,2048]{2,1,0:T(8,128)(2,1)} %bitcast.15, bf16[128,2048]{1,0:T(8,128)(2,1)} %bitcast.17, bf16[128,2048]{1,0:T(8,128)(2,1)} %last_in.1, ...), custom_call_target="tpu_custom_call" | custom-call | tf_op jit(solution)/shard_map/window/pallas_call | solution.py:777
  95.0 1.9 %copy.21 = bf16[1,128,2048]{2,1,0:T(8,128)(2,1)} copy(bf16[1,128,2048]{2,1,0:T(8,128)(2,1)} %bitcast.21) | data formatting | bytes 1048576
  96.9 1.9 %copy.22 = bf16[1,128,2048]{2,1,0:T(8,128)(2,1)} copy(bf16[1,128,2048]{2,1,0:T(8,128)(2,1)} %bitcast.20) | data formatting | bytes 1048576
  98.8 1.5 %copy.23 = f32[27,512]{1,0:T(8,128)} copy(f32[27,512]{1,0:T(8,128)} %get-tuple-element.14) | data formatting | bytes 110592
